TPU v7x, 32 devices: a whole 2x2x4 slice. The times are simulated.
32 devices in a mesh: gx: 8 (over y, x, core), gy: 4 (over z).
Axes of the slice: x: 2, y: 2, z: 4, core: 2. Of those that a mesh axis runs over, the one named last changes fastest.
Arguments:
- core_one: bfloat16 [200, 128], replicated, may hold values from -6 to 6
- core_two: bfloat16 [200, 4096], replicated, may hold values from -1 to 1
- core_three: bfloat16 [250, 256], replicated, may hold values from -1 to 1
- dense_rows: bfloat16 [2048, 128], P(('gx', 'gy')), may hold values from -6 to 6
- w_top: bfloat16 [256, 256], replicated, may hold values from -0.375 to 0.375
- bias_top: float32 [256], replicated, may hold values from -3 to 3
- w_out: float32 [256], replicated, may hold values from -0.75 to 0.75
- labels: int32 [2048], P(('gx', 'gy')), may hold values 0 or 1
- bag_ids: int32 [32, 256], P(('gx', 'gy')), may hold values from 0 to 63, never falling along the last dimension, each value on 1 to 8 neighbouring positions
- digit_one: int32 [32, 256], P(('gx', 'gy')), may hold values from 0 to 199
- digit_two: int32 [32, 256], P(('gx', 'gy')), may hold values from 0 to 199
- digit_three: int32 [32, 256], P(('gx', 'gy')), may hold values from 0 to 249
Outputs:
- core_grad: float32 [908800], P(('gx', 'gy'))
- top_grad: float32 [258, 256], replicated
Inputs may be any that keep to these rules, and one draw needn't show every extreme that they name: `bag_ids`: along a row, never falling; every sample of the block gets 1 to 8 lookups, one exactly 8.
All inputs are finite; a program needn't handle non-finite values. No bound on the sum of `labels` on one device may be relied on, other than what follows from the above.
Results may differ from a plain program's by a relative error of at most 0.0018.
The roundings to bfloat16 on the way count: a program that leaves them out, or rounds other values in their place, can miss the bound.
Values sent between devices are 32-bit elements; how exact they have to be, the bound alone decides.
A program may use at most 64 MiB of HBM per device.

v0:
```python
import jax
import jax.numpy as jnp
from jax import lax
from jax.sharding import PartitionSpec as P

D1 = 4
D2 = 4
D3 = 8
R = 32


def one_hot(digits, count, kind):
    return (digits[:, None] == jnp.arange(count, dtype=jnp.int32)[None, :]).astype(kind)


def slices(digits, core):
    return jnp.dot(
        one_hot(digits, core.shape[0], jnp.bfloat16), core, preferred_element_type=jnp.float32
    )


def factors(digits, cores):
    high = lax.Precision.HIGHEST
    first = slices(digits[0], cores[0]).reshape(-1, D1, R)
    middle = slices(digits[1], cores[1]).reshape(-1, R, D2 * R)
    last = slices(digits[2], cores[2]).reshape(-1, R, D3)
    left = jnp.einsum("nia,nab->nib", first, middle, precision=high).reshape(-1, D1 * D2, R)
    return (first, middle, last, left)


def top_total(top_local):
    return lax.psum(top_local, ("gx", "gy"))


def per_device(
    core_one,
    core_two,
    core_three,
    dense_rows,
    w_top,
    bias_top,
    w_out,
    labels,
    bag_ids,
    digit_one,
    digit_two,
    digit_three,
):
    high = lax.Precision.HIGHEST
    cores = (core_one, core_two, core_three)
    digits = jnp.stack([digit_one[0], digit_two[0], digit_three[0]])
    looks = digits.shape[1]
    block = min(256, looks)
    blocks = looks // block
    blocked = digits.reshape(3, blocks, block).transpose(1, 0, 2)
    width = D1 * D2 * D3

    def forward(carry, part):
        first, middle, last, left = factors(part, cores)
        return (carry, jnp.einsum("npa,nad->npd", left, last, precision=high).reshape(block, width))

    _, embedded = lax.scan(forward, jnp.zeros((), jnp.float32), blocked)
    embedded = embedded.reshape(looks, width)
    samples = dense_rows.shape[0]
    bag_table = one_hot(bag_ids[0], samples, jnp.float32)
    pooled = jnp.dot(bag_table.T, embedded, precision=high)
    joined = jnp.concatenate([dense_rows, pooled.astype(jnp.bfloat16)], axis=1)
    pre = jnp.dot(joined, w_top, preferred_element_type=jnp.float32) + bias_top[None, :]
    sig = jax.nn.sigmoid(pre)
    hidden = pre * sig
    logit = jnp.dot(hidden, w_out, precision=high)
    dlogit = (jax.nn.sigmoid(logit) - labels.astype(jnp.float32)) / samples
    dpre = dlogit[:, None] * w_out[None, :] * (sig * (1.0 + pre * (1.0 - sig)))
    dpre_low = dpre.astype(jnp.bfloat16)
    grad_weight = jnp.dot(joined.T, dpre_low, preferred_element_type=jnp.float32)
    grad_bias = jnp.sum(dpre, axis=0)
    grad_output = jnp.sum(hidden * dlogit[:, None], axis=0)
    top_local = jnp.concatenate([grad_weight, grad_bias[None, :], grad_output[None, :]], axis=0)
    grad_pooled = jnp.dot(dpre_low, w_top[width:].T, preferred_element_type=jnp.float32)
    grad_embedded = jnp.dot(bag_table, grad_pooled, precision=high).reshape(blocks, block, width)

    def backward(totals, inputs):
        part, grad_block = inputs
        first, middle, last, left = factors(part, cores)
        grad_view = grad_block.reshape(block, D1 * D2, D3)
        grad_last = jnp.einsum("npa,npd->nad", left, grad_view, precision=high)
        grad_left = jnp.einsum("npd,nad->npa", grad_view, last, precision=high).reshape(
            block, D1, D2 * R
        )
        grad_first = jnp.einsum("nib,nab->nia", grad_left, middle, precision=high)
        grad_middle = jnp.einsum("nia,nib->nab", first, grad_left, precision=high)
        pieces = (
            grad_first.reshape(block, -1),
            grad_middle.reshape(block, -1),
            grad_last.reshape(block, -1),
        )
        updated = tuple(
            (
                total
                + jnp.dot(
                    one_hot(part[number], cores[number].shape[0], jnp.float32).T,
                    pieces[number],
                    precision=high,
                )
                for number, total in enumerate(totals)
            )
        )
        return (updated, None)

    start = tuple((jnp.zeros(core.shape, jnp.float32) for core in cores))
    totals, _ = lax.scan(backward, start, (blocked, grad_embedded))
    flat = jnp.concatenate([total.reshape(-1) for total in totals])
    core_grad = lax.psum_scatter(flat, ("gx", "gy"), scatter_dimension=0, tiled=True)
    top_grad = top_total(top_local)
    return (core_grad, top_grad)


def solution(mesh):
    return jax.shard_map(
        per_device,
        mesh=mesh,
        in_specs=(
            P(),
            P(),
            P(),
            P(("gx", "gy"), None),
            P(),
            P(),
            P(),
            P(("gx", "gy")),
            P(("gx", "gy"), None),
            P(("gx", "gy"), None),
            P(("gx", "gy"), None),
            P(("gx", "gy"), None),
        ),
        out_specs=(P(("gx", "gy")), P()),
        check_vma=False,
    )
```

profile of v0, /device:TPU:0, one launch (start us, length us, event | category | flops | bytes accessed | tf_op | source)
XLA Modules:
  0.0 232.0 jit_solution(1863657441070256171)
XLA Ops:
  7.2 1.2 fusion.16
  8.4 0.2 copy.35
  8.7 1.2 convolution_bitcast_fusion.2
  9.9 0.4 copy.38
  10.4 1.4 convolution_bitcast_fusion.1
  11.8 0.8 copy.50
  12.6 1.9 copy-done.1
  14.5 4.2 %fusion.41 = f32[256,4,128]{2,1,0:T(4,128)} fusion(f32[256,4,32]{2,1,0:T(4,128)S(1)} %copy.35, f32[256,32,128]{2,1,0:T(8,128)S(1)} %bitcast.68), kind=kOutput, calls=%fused_computation.52 | convolution fusion | flops 50331648 | bytes 4849664 | tf_op jit(solution)/shard_map/while/body/eval_jaxpr/nia,nab->nib/dot_general | solution.py:27
  18.8 2.1 copy.36
  20.8 3.6 %copy.37 = f32[256,16,32]{2,1,0:T(8,128)} copy(f32[256,16,32]{0,2,1:T(8,128)} %bitcast.72) | data formatting | bytes 1048576 | tf_op jit(solution)/shard_map/while/body/eval_jaxpr/reshape | solution.py:27
  24.5 6.0 %fusion.42 = f32[256,16,8]{1,2,0:T(8,128)} fusion(f32[256,16,32]{2,1,0:T(8,128)} %copy.37, f32[256,32,8]{1,2,0:T(8,128)S(1)} %copy.38), kind=kOutput, calls=%fused_computation.53 | convolution fusion | flops 12582912 | bytes 917504 | tf_op jit(solution)/shard_map/while/body/eval_jaxpr/npa,nad->npd/dot_general | solution.py:60
  30.4 1.5 copy.39
  32.0 0.3 convolution_convert_fusion
  33.0 0.9 fusion.33
  33.9 0.3 convolution_bitcast_fusion.3
  34.2 1.4 copy.40
  35.6 5.1 %fusion.46 = f32[256,32,8]{1,2,0:T(8,128)} fusion(f32[256,16,32]{2,1,0:T(8,128)} %copy.37, f32[256,16,8]{1,2,0:T(8,128)} %copy.40), kind=kOutput, calls=%fused_computation.57 | convolution fusion | flops 12582912 | bytes 917504 | tf_op jit(solution)/shard_map/while/body/eval_jaxpr/npa,npd->nad/dot_general | solution.py:86
  40.8 4.8 %fusion.43 = f32[256,16,32]{2,1,0:T(8,128)} fusion(f32[256,16,8]{1,2,0:T(8,128)S(1)} %copy-done.2, f32[256,32,8]{1,2,0:T(8,128)S(1)} %copy.38), kind=kOutput, calls=%fused_computation.54 | convolution fusion | flops 12582912 | bytes 917504 | tf_op jit(solution)/shard_map/while/body/eval_jaxpr/npd,nad->npa/dot_general | solution.py:87
  45.6 2.5 %copy.42 = f32[256,16,32]{0,2,1:T(8,128)S(1)} copy(f32[256,16,32]{2,1,0:T(8,128)} %fusion.43) | data formatting | bytes 1048576 | tf_op jit(solution)/shard_map/while/body/eval_jaxpr/npd,nad->npa/dot_general | solution.py:87
  48.3 8.3 %fusion.44 = f32[256,4,32]{2,1,0:T(4,128)S(1)} fusion(f32[256,4,128]{2,1,0:T(4,128)S(1)} %copy.43, f32[256,32,128]{2,1,0:T(8,128)} %bitcast.69), kind=kOutput, calls=%fused_computation.55 | convolution fusion | flops 50331648 | bytes 4849664 | tf_op jit(solution)/shard_map/while/body/eval_jaxpr/nib,nab->nia/dot_general | solution.py:90
  56.6 8.3 %fusion.45 = f32[256,32,128]{2,1,0:T(8,128)} fusion(f32[256,4,32]{2,1,0:T(4,128)S(1)} %copy.35, f32[256,4,128]{2,1,0:T(4,128)S(1)} %copy.43), kind=kOutput, calls=%fused_computation.56 | convolution fusion | flops 50331648 | bytes 4849664 | tf_op jit(solution)/shard_map/while/body/eval_jaxpr/nia,nib->nab/dot_general | solution.py:91
  64.9 1.6 copy.49
  66.5 0.4 fusion.12
  67.1 0.3 convolution_bitcast_fusion
  67.5 6.6 %fusion.3 = f32[25,32,8,128]{3,2,1,0:T(8,128)S(1)} fusion(f32[32,8,32,128]{3,2,1,0:T(8,128)} %bitcast.70, s32[256]{0:T(256)S(1)} %bitcast.77), kind=kOutput, calls=%fused_computation.6 | convolution fusion | flops 2516633600 | bytes 7472128 | tf_op jit(solution)/shard_map/while/body/eval_jaxpr/dot_general | solution.py:100
  74.1 0.6 copy.52
  74.7 0.4 copy-done.3
  75.0 0.7 pad_maximum_fusion.1
  75.8 2.1 pad_maximum_fusion
  77.9 144.0 %all-reduce.4.cloned.1.call-done = (f32[908800]{0:T(1024)}, f32[258,256]{1,0:T(8,128)}) async-done(((f32[908800]{0:T(1024)}, f32[258,256]{1,0:T(8,128)}), (f32[908800]{0:T(1024)}, f32[258,256]{1,0:T(8,128)})) %all-reduce.4.cloned.1.call-update) | async-done | bytes 3899408
  221.9 1.6 dynamic-slice.2
  223.5 1.7 copy.61
  (33 shorter events, 1.2 us)
Async XLA Ops:
  7.2 3.2 %copy-start = (bf16[200,4096]{1,0:T(8,128)(2,1)S(1)}, bf16[200,4096]{1,0:T(8,128)(2,1)}, u32[]{:S(2)}) copy-start(bf16[200,4096]{1,0:T(8,128)(2,1)} %param.13) | copy-start | bytes 4915204
  7.2 214.7 %all-reduce.4.cloned.1.call-start = ((), (), s32[]{:S(2)}) async-start(), calls=%async_computation | async-start | bytes 7815168
  12.6 1.9 copy-start.1
  20.8 11.1 %copy-start.7 = (s32[1,256]{1,0:T(1,128)S(1)}, s32[1,256]{1,0:T(1,128)}, u32[]{:S(2)}) copy-start(s32[1,256]{1,0:T(1,128)} %param.20) | copy-start | bytes 3076
  20.8 11.5 %copy-start.4 = (bf16[256,256]{1,0:T(8,128)(2,1)S(1)}, bf16[256,256]{1,0:T(8,128)(2,1)}, u32[]{:S(2)}) copy-start(bf16[256,256]{1,0:T(8,128)(2,1)} %param.16) | copy-start | bytes 393220
  20.8 11.5 %copy-start.6 = (bf16[64,128]{1,0:T(8,128)(2,1)S(1)}, bf16[64,128]{1,0:T(8,128)(2,1)}, u32[]{:S(2)}) copy-start(bf16[64,128]{1,0:T(8,128)(2,1)} %param.15) | copy-start | bytes 49156
  20.8 11.5 %copy-start.10 = (f32[256]{0:T(256)S(1)}, f32[256]{0:T(256)}, u32[]{:S(2)}) copy-start(f32[256]{0:T(256)} %param.17) | copy-start | bytes 3076
  20.8 11.6 %copy-start.11 = (f32[256]{0:T(256)S(1)}, f32[256]{0:T(256)}, u32[]{:S(2)}) copy-start(f32[256]{0:T(256)} %param.18) | copy-start | bytes 3076
  20.8 11.6 %copy-start.12 = (s32[64]{0:T(128)S(1)}, s32[64]{0:T(128)}, u32[]{:S(2)}) copy-start(s32[64]{0:T(128)} %param.19) | copy-start | bytes 772
  35.6 5.1 %copy-start.2 = (f32[256,16,8]{1,2,0:T(8,128)S(1)}, f32[256,16,8]{1,2,0:T(8,128)}, u32[]{:S(2)}) copy-start(f32[256,16,8]{1,2,0:T(8,128)} %copy.40) | copy-start | bytes 393220
  56.6 9.9 %copy-start.8 = (s32[1,256]{1,0:T(1,128)S(1)}, s32[1,256]{1,0:T(1,128)}, u32[]{:S(2)}) copy-start(s32[1,256]{1,0:T(1,128)} %param.23) | copy-start | bytes 3076
  56.6 10.5 %copy-start.9 = (s32[1,256]{1,0:T(1,128)S(1)}, s32[1,256]{1,0:T(1,128)}, u32[]{:S(2)}) copy-start(s32[1,256]{1,0:T(1,128)} %param.21) | copy-start | bytes 3076
  56.6 10.8 %copy-start.5 = (s32[1,256]{1,0:T(1,128)S(1)}, s32[1,256]{1,0:T(1,128)}, u32[]{:S(2)}) copy-start(s32[1,256]{1,0:T(1,128)} %param.22) | copy-start | bytes 3076
  74.1 1.0 copy-start.3
Sparse Core Ops, SparseCore 0:
  78.0 143.8 all-reduce.3
where the time goes:
time: 233 us; the launch traced here: 232 us
  waiting for transfers between devices  144 us (62%)
  matrix products  50 us (21%)
  local copies, waits for them, and re-layouts  20.8 us (9%)
  between operations  14.3 us (6%)
  other arithmetic  2.92 us (1%)
    unnamed x2, waiting for transfers between devices  144 us
    dot_general x1, matrix products, backward(): grad_first = jnp.einsum('nib,nab->nia', grad_left, middle, precision=high)  8.32 us
    dot_general x1, matrix products, backward(): grad_middle = jnp.einsum('nia,nib->nab', first, grad_left, precision=high)  8.26 us
    dot_general x3, matrix products, backward(): jnp.dot(one_hot(part[number], cores[number].shape[0], jnp.float32).T, pie...  7.35 us
    unnamed x30, local copies, waits for them, and re-layouts  7.02 us
    dot_general x1, matrix products, forward(): jnp.einsum('npa,nad->npd', left, last, precision=high).reshape(block, width)  5.95 us
    dot_general x1, matrix products, backward(): grad_last = jnp.einsum('npa,npd->nad', left, grad_view, precision=high)  5.13 us
    dot_general x1, matrix products, backward(): jnp.einsum('npd,nad->npa', grad_view, last, precision=high)  4.8 us
  transfers between devices with their start and end apart: 1, of which 1 were waited for; matrix products, arithmetic and copies ran while one was open for 0% of the time, Pallas kernels for 0%

commit v1 on v0

--- a/solution.py
+++ b/solution.py
@@ -1,12 +1,280 @@
+import functools
+
 import jax
 import jax.numpy as jnp
 from jax import lax
+from jax.experimental import pallas as pl
+from jax.experimental.pallas import tpu as pltpu
 from jax.sharding import PartitionSpec as P
 
 D1 = 4
 D2 = 4
 D3 = 8
 R = 32
+WIDTH = D1 * D2 * D3
+PAIRS = D1 * D2
+SIDE = D2 * R
+AXES = ("gx", "gy")
+F32 = jnp.float32
+BF16 = jnp.bfloat16
+HIGH = lax.Precision.HIGHEST
+
+
+def dot(a, b, dims, precision=None):
+    return lax.dot_general(
+        a, b, (dims, ((), ())), precision=precision, preferred_element_type=F32
+    )
+
+
+def hot(row, count, kind):
+    numbers = lax.broadcasted_iota(jnp.int32, (count, row.shape[1]), 0)
+    return jnp.where(numbers == row, 1.0, 0.0).astype(kind)
+
+
+def by_d3(last_t):
+    size = R * D3
+    to = lax.broadcasted_iota(jnp.int32, (size, size), 0)
+    of = lax.broadcasted_iota(jnp.int32, (size, size), 1)
+    turn = jnp.where(of == (to % R) * D3 + to // R, 1.0, 0.0).astype(BF16)
+    return dot(turn, last_t, ((1,), (0,)))
+
+
+def grad_left_into(gleft_s, g_s, lastd_s):
+    @pl.loop(0, PAIRS)
+    def _(p):
+        total = None
+        for d in range(D3):
+            term = g_s[pl.ds(p * D3 + d, 1), :] * lastd_s[d * R:(d + 1) * R, :]
+            total = term if total is None else total + term
+        gleft_s[pl.ds(pl.multiple_of(p * R, R), R), :] = total
+
+
+def local_kernel(
+    c1, c2, c3, dense, w, bias, wout, labels, bag, d1, d2, d3,
+    gp_ref, gw_ref, gv_ref, gf_ref, gl_ref,
+    mid_s, first_s, last_s, lastd_s, left_s, gleft_s, emb_s, g_s, gf_s, gl_s,
+):
+    samples = dense.shape[0]
+    looks = d1.shape[1]
+    hot1 = hot(d1[...], c1.shape[0], BF16)
+    hot2 = hot(d2[...], c2.shape[0], BF16)
+    hot3 = hot(d3[...], c3.shape[0], BF16)
+    down = ((0,), (0,))
+    across = ((1,), (1,))
+    plain = ((1,), (0,))
+    for start in range(0, R * SIDE, 512):
+        mid_s[start:start + 512, :] = dot(c2[:, start:start + 512], hot2, down)
+    first_s[...] = dot(c1[...], hot1, down)
+    last_t = dot(c3[...], hot3, down)
+    last_s[...] = last_t
+    lastd_s[...] = by_d3(last_t.astype(BF16))
+
+    lane_blocks = looks // 128
+
+    @pl.loop(0, D2 * lane_blocks)
+    def _(step):
+        j = step // lane_blocks
+        lanes = pl.ds(pl.multiple_of((step % lane_blocks) * 128, 128), 128)
+        totals = [None] * D1
+        for a in range(R):
+            m = mid_s[pl.ds(pl.multiple_of(a * SIDE + j * R, R), R), lanes]
+            for i in range(D1):
+                term = first_s[i * R + a:i * R + a + 1, lanes] * m
+                totals[i] = term if totals[i] is None else totals[i] + term
+        for i in range(D1):
+            left_s[pl.ds(pl.multiple_of(i * SIDE + j * R, R), R), lanes] = totals[i]
+
+    @pl.loop(0, PAIRS)
+    def _(p):
+        totals = [None, None]
+        for c in range(R):
+            term = left_s[pl.ds(p * R + c, 1), :] * last_s[c * D3:(c + 1) * D3, :]
+            k = c % 2
+            totals[k] = term if totals[k] is None else totals[k] + term
+        emb_s[pl.ds(pl.multiple_of(p * D3, D3), D3), :] = totals[0] + totals[1]
+
+    bags = hot(bag[...], samples, F32)
+    pooled = dot(bags, emb_s[...], across, HIGH).astype(BF16)
+    pre = (
+        dot(dense[...], w[:WIDTH, :], plain) + dot(pooled, w[WIDTH:, :], plain)
+        + bias[...]
+    )
+    sig = jax.nn.sigmoid(pre)
+    hidden = pre * sig
+    logit = jnp.sum(hidden * wout[...], axis=1, keepdims=True)
+    rows = lax.broadcasted_iota(jnp.int32, (samples, samples), 0)
+    cols = lax.broadcasted_iota(jnp.int32, (samples, samples), 1)
+    label = jnp.sum(
+        jnp.where(rows == cols, labels[...].astype(F32), 0.0), axis=1, keepdims=True
+    )
+    dlogit = (jax.nn.sigmoid(logit) - label) / samples
+    dpre = dlogit * wout[...] * (sig * (1.0 + pre * (1.0 - sig)))
+    low = dpre.astype(BF16)
+    gw_ref[:WIDTH, :] = dot(dense[...], low, down)
+    gw_ref[WIDTH:, :] = dot(pooled, low, down)
+    gv_ref[0:1, :] = jnp.sum(dpre, axis=0, keepdims=True)
+    gv_ref[1:2, :] = jnp.sum(hidden * dlogit, axis=0, keepdims=True)
+    gp = dot(low, w[WIDTH:, :], across)
+    gp_ref[...] = gp
+    g_s[...] = dot(gp, bags, down, HIGH)
+
+    grad_left_into(gleft_s, g_s, lastd_s)
+
+    @pl.loop(0, R)
+    def _(c):
+        totals = [None, None]
+        for p in range(PAIRS):
+            term = left_s[pl.ds(p * R + c, 1), :] * g_s[p * D3:(p + 1) * D3, :]
+            k = p % 2
+            totals[k] = term if totals[k] is None else totals[k] + term
+        gl_s[pl.ds(pl.multiple_of(c * D3, D3), D3), :] = totals[0] + totals[1]
+
+    @pl.loop(0, R)
+    def _(a):
+        totals = [None] * D1
+        for t in range(0, SIDE, 8):
+            m = mid_s[pl.ds(pl.multiple_of(a * SIDE + t, 8), 8), :]
+            for i in range(D1):
+                term = gleft_s[i * SIDE + t:i * SIDE + t + 8, :] * m
+                totals[i] = term if totals[i] is None else totals[i] + term
+        for i in range(D1):
+            gf_s[pl.ds(i * R + a, 1), :] = jnp.sum(totals[i], axis=0, keepdims=True)
+
+    gf_ref[...] = dot(hot1.astype(F32), gf_s[...], across, HIGH)
+    gl_ref[...] = dot(hot3.astype(F32), gl_s[...], across, HIGH)
+
+
+def local_part(c1, c2, c3, dense, w, bias, wout, labels, bag, d1, d2, d3):
+    samples, looks = dense.shape[0], d1.shape[1]
+    shape = lambda *dims: jax.ShapeDtypeStruct(dims, F32)
+    scratch = [R * SIDE, D1 * R, R * D3, R * D3, D1 * SIDE, D1 * SIDE, WIDTH, WIDTH, D1 * R, R * D3]
+    return pl.pallas_call(
+        local_kernel,
+        out_shape=(
+            shape(samples, WIDTH), shape(*w.shape), shape(2, w.shape[1]),
+            shape(*c1.shape), shape(*c3.shape),
+        ),
+        scratch_shapes=[pltpu.VMEM((rows, looks), F32) for rows in scratch],
+        compiler_params=pltpu.CompilerParams(vmem_limit_bytes=40 << 20),
+        name="local",
+    )(c1, c2, c3, dense, w, bias, wout, labels, bag, d1, d2, d3)
+
+
+def middle_kernel(
+    window, chunk, r0_ref, c1, c3, gp, digits, out_ref,
+    rank_s, vals_s, g_s, lastd_s, gleft_s,
+):
+    groups, looks = digits.shape[1:]
+    samples = gp.shape[0] // groups
+    r0 = r0_ref[0]
+    rel = digits[2] - r0
+    inside = (rel >= 0) & (rel < window)
+    mask = jnp.where(inside, 1.0, 0.0)
+    low = mask.astype(BF16)
+    tri = jnp.where(
+        lax.broadcasted_iota(jnp.int32, (looks, looks), 0)
+        < lax.broadcasted_iota(jnp.int32, (looks, looks), 1), 1.0, 0.0).astype(BF16)
+    above = jnp.where(
+        lax.broadcasted_iota(jnp.int32, (groups, groups), 0)
+        > lax.broadcasted_iota(jnp.int32, (groups, groups), 1), 1.0, 0.0).astype(BF16)
+    plain, across, down = ((1,), (0,)), ((1,), (1,)), ((0,), (0,))
+    before = jnp.sum(dot(above, low, plain), axis=1, keepdims=True)
+    rank_s[...] = jnp.where(inside, dot(low, tri, plain) + before, -1.0).astype(jnp.int32)
+    count = jnp.sum(jnp.where(inside, 1, 0))
+    group = lax.broadcasted_iota(jnp.int32, (groups, looks), 0)
+    columns = (digits[0], digits[1], digits[3], group, jnp.where(inside, rel + 1, 0))
+    for k, column in enumerate(columns):
+        vals_s[:, k:k + 1, :] = column.astype(F32).reshape(groups, 1, looks)
+    vals_s[:, len(columns):, :] = jnp.zeros((groups, 8 - len(columns), looks), F32)
+    out_ref[...] = jnp.zeros_like(out_ref)
+    gp_high = gp[...].astype(BF16)
+    gp_low = (gp[...] - gp_high.astype(F32)).astype(BF16)
+    slots = lax.broadcasted_iota(jnp.int32, (chunk, looks), 0)
+
+    def body(step, carry):
+        def pick(e, found):
+            ranks = rank_s[pl.ds(e, 1), :] - step * chunk
+            chosen = jnp.where(slots == ranks, 1.0, 0.0).astype(BF16)
+            return found + dot(vals_s[e].astype(BF16), chosen, across)
+
+        found = lax.fori_loop(0, groups, pick, jnp.zeros((8, chunk), F32), unroll=4)
+        found = found.astype(jnp.int32)
+        bag, d1, d3, owner, rel1 = (found[k:k + 1, :] for k in range(5))
+        first = dot(c1[...], hot(d1, c1.shape[0], BF16), down)
+        last = dot(c3[...], hot(d3, c3.shape[0], BF16), down)
+        lastd_s[...] = by_d3(last.astype(BF16))
+        sample = hot(owner * samples + bag, gp.shape[0], BF16)
+        g_s[...] = dot(gp_high, sample, down) + dot(gp_low, sample, down)
+        grad_left_into(gleft_s, g_s, lastd_s)
+        total = out_ref[...]
+        for i in range(D1):
+            part = first[i * R:(i + 1) * R, :]
+            spread = jnp.concatenate(
+                [jnp.where(rel1 == r + 1, part, 0.0) for r in range(window)], axis=0
+            ).astype(BF16)
+            wide = gleft_s[i * SIDE:(i + 1) * SIDE, :]
+            high = wide.astype(BF16)
+            rest = (wide - high.astype(F32)).astype(BF16)
+            total = total + dot(spread, high, across) + dot(spread, rest, across)
+        out_ref[...] = total
+        return carry
+
+    lax.fori_loop(0, (count + chunk - 1) // chunk, body, 0)
+
+
+def middle_part(window, r0, c1, c3, gp, digits):
+    groups, looks = digits.shape[1:]
+    chunk = 512
+    vmem = pl.BlockSpec(memory_space=pltpu.VMEM)
+    return pl.pallas_call(
+        functools.partial(middle_kernel, window, chunk),
+        out_shape=jax.ShapeDtypeStruct((window * R, SIDE), F32),
+        in_specs=[pl.BlockSpec(memory_space=pltpu.SMEM), vmem, vmem, vmem, vmem],
+        out_specs=vmem,
+        scratch_shapes=[
+            pltpu.VMEM((groups, looks), jnp.int32),
+            pltpu.VMEM((groups, 8, looks), F32),
+            pltpu.VMEM((WIDTH, chunk), F32),
+            pltpu.VMEM((R * D3, chunk), F32),
+            pltpu.VMEM((D1 * SIDE, chunk), F32),
+        ],
+        compiler_params=pltpu.CompilerParams(vmem_limit_bytes=40 << 20),
+        name="middle",
+    )(r0, c1, c3, gp, digits)
+
+
+def cut(start, share, core_shapes, window, r0, first_sum, middle_rows, last_sum):
+    n1 = core_shapes[0][0] * core_shapes[0][1]
+    row = core_shapes[1][1]
+    n2 = core_shapes[1][0] * row
+    own_first = lax.dynamic_slice(
+        jnp.pad(first_sum, (0, share)), (jnp.minimum(start, n1),), (share,))
+    own_middle = lax.dynamic_slice(
+        jnp.pad(middle_rows, (share, share)),
+        (jnp.clip(start - n1 - r0 * row + share, 0, share + window * row),), (share,))
+    own_last = lax.dynamic_slice(
+        jnp.pad(last_sum, (share, 0)),
+        (jnp.clip(start - n1 - n2 + share, 0, last_sum.shape[0]),), (share,))
+    return own_first + own_middle + own_last
+
+
+def per_device(devices, c1, c2, c3, dense, w, bias, wout, labels, bag, d1, d2, d3):
+    total = c1.size + c2.size + c3.size
+    share = total // devices
+    row = c2.shape[1]
+    window = min(-(-share // row) + 1, c2.shape[0])
+    me = lax.axis_index(AXES)
+    start = me * share
+    r0 = jnp.clip((start - c1.size) // row, 0, c2.shape[0] - window)
+    digits = lax.all_gather(jnp.stack([bag, d1, d2, d3]), AXES, axis=1, tiled=True)
+    gp, gw, gv, gf, gl = local_part(
+        c1, c2, c3, dense, w, bias[None], wout[None], labels[None], bag, d1, d2, d3)
+    gp_all = lax.all_gather(gp, AXES, axis=0, tiled=True)
+    gw, gv, gf, gl = lax.psum((gw, gv, gf, gl), AXES)
+    rows = middle_part(window, r0[None], c1, c3, gp_all, digits)
+    core = cut(start, share, (c1.shape, c2.shape, c3.shape), window, r0,
+               gf.reshape(-1), rows.reshape(-1), gl.reshape(-1))
+    return core, jnp.concatenate([gw, gv], axis=0)
 
 
 def one_hot(digits, count, kind):
@@ -32,7 +300,7 @@
     return lax.psum(top_local, ("gx", "gy"))
 
 
-def per_device(
+def per_device_dense(
     core_one,
     core_two,
     core_three,
@@ -116,23 +384,24 @@
 
 
 def solution(mesh):
-    return jax.shard_map(
-        per_device,
-        mesh=mesh,
-        in_specs=(
-            P(),
-            P(),
-            P(),
-            P(("gx", "gy"), None),
-            P(),
-            P(),
-            P(),
-            P(("gx", "gy")),
-            P(("gx", "gy"), None),
-            P(("gx", "gy"), None),
-            P(("gx", "gy"), None),
-            P(("gx", "gy"), None),
-        ),
-        out_specs=(P(("gx", "gy")), P()),
-        check_vma=False,
-    )
+    devices = mesh.shape["gx"] * mesh.shape["gy"]
+    whole, split, rows = P(), P(AXES), P(AXES, None)
+
+    def step(*args):
+        cores, dense = args[:3], args[3]
+        if dense.size < sum(core.size for core in cores):
+            body = functools.partial(per_device, devices)
+        else:
+            body = per_device_dense
+        return jax.shard_map(
+            body,
+            mesh=mesh,
+            in_specs=(
+                whole, whole, whole, rows, whole, whole, whole, split,
+                rows, rows, rows, rows,
+            ),
+            out_specs=(split, whole),
+            check_vma=False,
+        )(*args)
+
+    return step

time: 233 us -> 232 us (level)
  blocking collectives: 0 us -> 108 us
  waiting for transfers between devices: 144 us -> 79.8 us
  matrix products: 50 us -> 0 us
  Pallas kernels: 0 us -> 15.1 us
  local copies, waits for them, and re-layouts: 20.8 us -> 11.5 us
    unnamed x2, waiting for transfers between devices: 144 us -> 0.71 us
    all_gather x0 -> x1, blocking collectives: none -> 70.9 us  [per_device(): lax.all_gather(jnp.stack([bag, d1, d2, d3]), AXES, axis=1, tiled=True)]
    all_gather x0 -> x1, waiting for transfers between devices: none -> 55.1 us  [per_device(): gp_all = lax.all_gather(gp, AXES, axis=0, tiled=True)]
    dot_general x18 -> x0, matrix products: 50 us -> none  [the longest x1 8.32 us: backward(): grad_first = jnp.einsum('nib,nab->nia', grad_left, middle, precision=high)]
    psum x0 -> x1, blocking collectives: none -> 36.9 us  [per_device(): gw, gv, gf, gl = lax.psum((gw, gv, gf, gl), AXES)]
    psum x0 -> x1, waiting for transfers between devices: none -> 24 us  [per_device(): gw, gv, gf, gl = lax.psum((gw, gv, gf, gl), AXES)]
    pallas_call x0 -> x2, Pallas kernels: none -> 15.1 us  [the longest x1 8.78 us: local_part(): pl.pallas_call(local_kernel, out_shape=(shape(samples, WIDTH), shape(*w.s...]
    dot_general x5 -> x0, local copies, waits for them, and re-layouts: 7.84 us -> none  [the longest x1 2.49 us: backward(): jnp.einsum('npd,nad->npa', grad_view, last, precision=high)]
  transfers between devices with their start and end apart: 1 -> 2, of which waited for: 1 -> 2; matrix products, arithmetic and copies ran while one was open for 0% -> 1% of each run, Pallas kernels for 0% -> 0%
where the time goes in v1:
time: 232 us; the launch traced here: 231 us
  blocking collectives  108 us (47%)
  waiting for transfers between devices  79.8 us (34%)
  Pallas kernels  15.1 us (7%)
  between operations  14.2 us (6%)
  local copies, waits for them, and re-layouts  11.5 us (5%)
  other arithmetic  2.62 us (1%)
    all_gather x1, blocking collectives, per_device(): lax.all_gather(jnp.stack([bag, d1, d2, d3]), AXES, axis=1, tiled=True)  70.9 us
    all_gather x1, waiting for transfers between devices, per_device(): gp_all = lax.all_gather(gp, AXES, axis=0, tiled=True)  55.1 us
    psum x1, blocking collectives, per_device(): gw, gv, gf, gl = lax.psum((gw, gv, gf, gl), AXES)  36.9 us
    psum x1, waiting for transfers between devices, per_device(): gw, gv, gf, gl = lax.psum((gw, gv, gf, gl), AXES)  24 us
    unnamed x42, local copies, waits for them, and re-layouts  10.7 us
    pallas_call x1, Pallas kernels, local_part(): pl.pallas_call(local_kernel, out_shape=(shape(samples, WIDTH), shape(*w.s...  8.78 us
    pallas_call x1, Pallas kernels, middle_part(): pl.pallas_call(functools.partial(middle_kernel, window, chunk), out_shape...  6.31 us
  transfers between devices with their start and end apart: 2, of which 2 were waited for; matrix products, arithmetic and copies ran while one was open for 1% of the time, Pallas kernels for 0%

profile of v1, /device:TPU:0, one launch (start us, length us, event | category | flops | bytes accessed | tf_op | source)
XLA Modules:
  0.0 231.1 jit_solution(16825798105070531167)
XLA Ops:
  7.2 0.0 copy-start.9
  7.2 0.0 copy-start.11
  7.2 0.0 copy-start.13
  7.2 0.0 copy-start.15
  7.2 0.0 all-reduce.6.cloned.1.call-start
  7.3 0.0 copy-start
  7.3 1.4 copy-done
  8.7 0.9 copy-done.2
  9.6 0.8 copy-done.4
  10.4 0.9 copy-done.6
  11.3 0.7 copy-done.7
  12.0 0.7 copy-done.8
  12.7 0.7 copy-done.10
  13.4 0.7 copy-done.12
  14.1 0.7 copy-done.14
  14.7 0.7 copy-done.16
  15.4 0.7 copy-done.17
  16.1 0.7 copy-done.18
  16.8 8.8 %local.1 = (f32[64,128]{1,0:T(8,128)}, f32[256,256]{1,0:T(8,128)}, f32[2,256]{1,0:T(2,128)S(1)}, f32[200,128]{1,0:T(8,128)}, f32[250,256]{1,0:T(8,128)S(1)}) custom-call(bf16[200,128]{1,0:T(8,128)(2,1)S(1)} %copy-done.4, bf16[200,4096]{1,0:T(8,128)(2,1)S(1)} %copy-done, bf16[250,256]{1,0:T(8,128)(2,1)S(1)} %copy-done.2, bf16[64,128]{1,0:T(8,128)(2,1)S(1)} %copy-done.7, ...), custom_call_target="tpu_custom_call" | custom-call | tf_op jit(solution)/shard_map/local/pallas_call | solution.py:151
  25.5 0.7 reshape.15
  26.3 0.0 all-reduce.6.cloned.1.call-update
  26.3 0.0 all-gather.2.cloned.1.call-start
  26.3 0.7 all-gather.2.cloned.1.call-update
  27.1 70.9 %all_gather.7 = s32[4,32,256]{2,0,1:T(4,128)S(1)} all-gather(s32[4,1,256]{2,0,1:T(4,128)S(1)} %pad_add_fusion), channel_id=1, replica_groups=mesh['gx'=8,'gy'=4] {'gx','gy'}, dimensions={1}, use_global_device_ids=true | all-gather | bytes 135168 | tf_op jit(solution)/shard_map/all_gather | solution.py:269
  98.1 36.9 %psum.31 = f32[2,256]{1,0:T(2,128)S(1)} all-reduce(f32[2,256]{1,0:T(2,128)S(1)} %get-tuple-element.11), channel_id=1, replica_groups=mesh['gx'=8,'gy'=4] {'gx','gy'}, use_global_device_ids=true, to_apply=%region_3.4 | all-reduce | flops 512 | bytes 4096 | tf_op jit(solution)/shard_map/psum | solution.py:273
  135.0 24.0 %all-reduce.6.cloned.1.call-done = (f32[25600]{0:T(1024)}, f32[64000]{0:T(1024)}, f32[256,256]{1,0:T(8,128)}) async-done(((f32[25600]{0:T(1024)}, f32[64000]{0:T(1024)}, f32[256,256]{1,0:T(8,128)}), (f32[25600]{0:T(1024)}, f32[64000]{0:T(1024)}, f32[256,256]{1,0:T(8,128)})) %all-reduce.6.cloned.1.call-update) | async-done | bytes 620560 | tf_op jit(solution)/shard_map/psum | solution.py:273
  159.0 1.7 pad_maximum_fusion
  160.8 55.1 %all-gather.2.cloned.1.call-done.gp = f32[2048,128]{1,0:T(8,128)} async-done(((f32[64,128]{1,0:T(8,128)}), f32[2048,128]{1,0:T(8,128)}) %all-gather.2.cloned.1.call-update) | async-done | bytes 1048592 | tf_op jit(solution)/shard_map/all_gather | solution.py:272
  215.8 0.0 copy-done.3
  215.8 1.2 copy-done.1
  217.1 6.3 %middle.1 = f32[256,128]{1,0:T(8,128)S(1)} custom-call(s32[1]{0:T(128)} %bitcast.4.r0_ref, bf16[200,128]{1,0:T(8,128)(2,1)S(1)} %copy-done.5, bf16[250,256]{1,0:T(8,128)(2,1)S(1)} %copy-done.3, f32[2048,128]{1,0:T(8,128)S(1)} %copy-done.1, s32[4,32,256]{2,1,0:T(8,128)S(1)} %copy.14.digits), custom_call_target="tpu_custom_call" | custom-call | tf_op jit(solution)/shard_map/middle/pallas_call | solution.py:229
  223.4 0.9 fusion.1
  (25 shorter events, 0.1 us)
Async XLA Ops:
  7.2 19.9 %copy-start.9 = (s32[1,256]{1,0:T(1,128)S(1)}, s32[1,256]{1,0:T(1,128)}, u32[]{:S(2)}) copy-start(s32[1,256]{1,0:T(1,128)} %bag.1) | copy-start | bytes 3076
  7.2 19.9 %copy-start.11 = (s32[1,256]{1,0:T(1,128)S(1)}, s32[1,256]{1,0:T(1,128)}, u32[]{:S(2)}) copy-start(s32[1,256]{1,0:T(1,128)} %d1.1) | copy-start | bytes 3076
  7.2 19.9 %copy-start.13 = (s32[1,256]{1,0:T(1,128)S(1)}, s32[1,256]{1,0:T(1,128)}, u32[]{:S(2)}) copy-start(s32[1,256]{1,0:T(1,128)} %d2.1) | copy-start | bytes 3076
  7.2 19.9 %copy-start.15 = (s32[1,256]{1,0:T(1,128)S(1)}, s32[1,256]{1,0:T(1,128)}, u32[]{:S(2)}) copy-start(s32[1,256]{1,0:T(1,128)} %d3.1) | copy-start | bytes 3076
  7.2 151.8 %all-reduce.6.cloned.1.call-start = ((), (), s32[]{:S(2)}) async-start(), calls=%async_computation.1 | async-start | bytes 1245184 | tf_op jit(solution)/shard_map/psum | solution.py:273
  7.3 1.4 copy-start
  8.7 0.9 copy-start.2
  9.6 0.8 copy-start.4
  10.4 0.9 copy-start.6
  11.3 0.7 copy-start.7
  12.0 0.7 copy-start.8
  12.7 0.7 copy-start.10
  13.4 0.7 copy-start.12
  14.1 0.7 copy-start.14
  14.7 0.7 copy-start.16
  15.4 0.7 copy-start.17
  16.1 0.7 copy-start.18
  16.8 199.1 %copy-start.3 = (bf16[250,256]{1,0:T(8,128)(2,1)S(1)}, bf16[250,256]{1,0:T(8,128)(2,1)}, u32[]{:S(2)}) copy-start(bf16[250,256]{1,0:T(8,128)(2,1)} %c3.3) | copy-start | bytes 384004
  16.8 199.1 %copy-start.5 = (bf16[200,128]{1,0:T(8,128)(2,1)S(1)}, bf16[200,128]{1,0:T(8,128)(2,1)}, u32[]{:S(2)}) copy-start(bf16[200,128]{1,0:T(8,128)(2,1)} %c1.3) | copy-start | bytes 153604
  26.3 189.5 %all-gather.2.cloned.1.call-start = ((), (), s32[]{:S(2)}) async-start(), calls=%async_computation | async-start | bytes 1081344 | tf_op jit(solution)/shard_map/all_gather | solution.py:272
  159.0 64.3 %copy-start.19 = (f32[64000]{0:T(1024)S(1)}, f32[64000]{0:T(1024)}, u32[]{:S(2)}) copy-start(f32[64000]{0:T(1024)} %get-tuple-element.13) | copy-start | bytes 768004
  159.0 64.4 %copy-start.20 = (f32[25600]{0:T(1024)S(1)}, f32[25600]{0:T(1024)}, u32[]{:S(2)}) copy-start(f32[25600]{0:T(1024)} %get-tuple-element.12) | copy-start | bytes 307204
  215.8 1.2 copy-start.1
Sparse Core Ops, SparseCore 0:
  26.4 132.5 all-reduce.5
  162.0 53.7 all-gather.1

commit v2 on v1

--- a/solution.py
+++ b/solution.py
@@ -39,6 +39,22 @@
     return dot(turn, last_t, ((1,), (0,)))
 
 
+def up(count, step):
+    return -(-count // step) * step
+
+
+def places_of(shape_one, shape_three, shape_top):
+    places, at = {}, 0
+    shapes = dict(
+        weight=shape_top, first=shape_one, last=shape_three, vectors=(2, shape_top[1]))
+    for name, (rows, columns) in shapes.items():
+        places[name] = []
+        for _ in range(columns // 128):
+            places[name].append(at)
+            at += up(rows, 8)
+    return places, at
+
+
 def grad_left_into(gleft_s, g_s, lastd_s):
     @pl.loop(0, PAIRS)
     def _(p):
@@ -51,7 +67,7 @@
 
 def local_kernel(
     c1, c2, c3, dense, w, bias, wout, labels, bag, d1, d2, d3,
-    gp_ref, gw_ref, gv_ref, gf_ref, gl_ref,
+    block_ref, sums_ref,
     mid_s, first_s, last_s, lastd_s, left_s, gleft_s, emb_s, g_s, gf_s, gl_s,
 ):
     samples = dense.shape[0]
@@ -110,12 +126,25 @@
     dlogit = (jax.nn.sigmoid(logit) - label) / samples
     dpre = dlogit * wout[...] * (sig * (1.0 + pre * (1.0 - sig)))
     low = dpre.astype(BF16)
-    gw_ref[:WIDTH, :] = dot(dense[...], low, down)
-    gw_ref[WIDTH:, :] = dot(pooled, low, down)
-    gv_ref[0:1, :] = jnp.sum(dpre, axis=0, keepdims=True)
-    gv_ref[1:2, :] = jnp.sum(hidden * dlogit, axis=0, keepdims=True)
+    places, _ = places_of(c1.shape, c3.shape, w.shape)
+    sums_ref[...] = jnp.zeros_like(sums_ref)
+
+    def put(name, row, value):
+        for h in range(value.shape[1] // 128):
+            at = places[name][h] + row
+            sums_ref[at:at + value.shape[0], :] = value[:, h * 128:(h + 1) * 128]
+
+    put("weight", 0, dot(dense[...], low, down))
+    put("weight", WIDTH, dot(pooled, low, down))
+    put("vectors", 0, jnp.sum(dpre, axis=0, keepdims=True))
+    put("vectors", 1, jnp.sum(hidden * dlogit, axis=0, keepdims=True))
     gp = dot(low, w[WIDTH:, :], across)
-    gp_ref[...] = gp
+    block_ref[:samples, :] = gp
+    block_ref[samples:, :] = jnp.zeros((block_ref.shape[0] - samples, 128), F32)
+    for k, digit in enumerate((bag, d1, d2, d3)):
+        for h in range(looks // 128):
+            at = samples + k * (looks // 128) + h
+            block_ref[at:at + 1, :] = digit[:, h * 128:(h + 1) * 128].astype(F32)
     g_s[...] = dot(gp, bags, down, HIGH)
 
     grad_left_into(gleft_s, g_s, lastd_s)
@@ -140,19 +169,19 @@
         for i in range(D1):
             gf_s[pl.ds(i * R + a, 1), :] = jnp.sum(totals[i], axis=0, keepdims=True)
 
-    gf_ref[...] = dot(hot1.astype(F32), gf_s[...], across, HIGH)
-    gl_ref[...] = dot(hot3.astype(F32), gl_s[...], across, HIGH)
-
-
-def local_part(c1, c2, c3, dense, w, bias, wout, labels, bag, d1, d2, d3):
+    put("first", 0, dot(hot1.astype(F32), gf_s[...], across, HIGH))
+    put("last", 0, dot(hot3.astype(F32), gl_s[...], across, HIGH))
+
+
+def local_part(devices, c1, c2, c3, dense, w, bias, wout, labels, bag, d1, d2, d3):
     samples, looks = dense.shape[0], d1.shape[1]
     shape = lambda *dims: jax.ShapeDtypeStruct(dims, F32)
     scratch = [R * SIDE, D1 * R, R * D3, R * D3, D1 * SIDE, D1 * SIDE, WIDTH, WIDTH, D1 * R, R * D3]
     return pl.pallas_call(
         local_kernel,
         out_shape=(
-            shape(samples, WIDTH), shape(*w.shape), shape(2, w.shape[1]),
-            shape(*c1.shape), shape(*c3.shape),
+            shape(samples + up(4 * looks // 128, 8), WIDTH),
+            shape(up(places_of(c1.shape, c3.shape, w.shape)[1], 8 * devices), 128),
         ),
         scratch_shapes=[pltpu.VMEM((rows, looks), F32) for rows in scratch],
         compiler_params=pltpu.CompilerParams(vmem_limit_bytes=40 << 20),
@@ -161,11 +190,18 @@
 
 
 def middle_kernel(
-    window, chunk, r0_ref, c1, c3, gp, digits, out_ref,
+    window, chunk, samples, looks, r0_ref, c1, c3, blocks, out_ref,
     rank_s, vals_s, g_s, lastd_s, gleft_s,
 ):
-    groups, looks = digits.shape[1:]
-    samples = gp.shape[0] // groups
+    groups = blocks.shape[0]
+    gp = blocks[:, :samples, :].reshape(groups * samples, WIDTH)
+    per = looks // 128
+    digits = [
+        jnp.concatenate(
+            [blocks[:, samples + k * per + h, :] for h in range(per)], axis=1
+        ).astype(jnp.int32)
+        for k in range(4)
+    ]
     r0 = r0_ref[0]
     rel = digits[2] - r0
     inside = (rel >= 0) & (rel < window)
@@ -187,8 +223,8 @@
         vals_s[:, k:k + 1, :] = column.astype(F32).reshape(groups, 1, looks)
     vals_s[:, len(columns):, :] = jnp.zeros((groups, 8 - len(columns), looks), F32)
     out_ref[...] = jnp.zeros_like(out_ref)
-    gp_high = gp[...].astype(BF16)
-    gp_low = (gp[...] - gp_high.astype(F32)).astype(BF16)
+    gp_high = gp.astype(BF16)
+    gp_low = (gp - gp_high.astype(F32)).astype(BF16)
     slots = lax.broadcasted_iota(jnp.int32, (chunk, looks), 0)
 
     def body(step, carry):
@@ -222,14 +258,14 @@
     lax.fori_loop(0, (count + chunk - 1) // chunk, body, 0)
 
 
-def middle_part(window, r0, c1, c3, gp, digits):
-    groups, looks = digits.shape[1:]
+def middle_part(window, samples, looks, r0, c1, c3, blocks):
+    groups = blocks.shape[0]
     chunk = 512
     vmem = pl.BlockSpec(memory_space=pltpu.VMEM)
     return pl.pallas_call(
-        functools.partial(middle_kernel, window, chunk),
+        functools.partial(middle_kernel, window, chunk, samples, looks),
         out_shape=jax.ShapeDtypeStruct((window * R, SIDE), F32),
-        in_specs=[pl.BlockSpec(memory_space=pltpu.SMEM), vmem, vmem, vmem, vmem],
+        in_specs=[pl.BlockSpec(memory_space=pltpu.SMEM), vmem, vmem, vmem],
         out_specs=vmem,
         scratch_shapes=[
             pltpu.VMEM((groups, looks), jnp.int32),
@@ -240,7 +276,80 @@
         ],
         compiler_params=pltpu.CompilerParams(vmem_limit_bytes=40 << 20),
         name="middle",
-    )(r0, c1, c3, gp, digits)
+    )(r0, c1, c3, blocks)
+
+
+def exchange_kernel(
+    nx, ny, block, sums, blocks_ref, total_ref,
+    parts, send_a, recv_a, send_b, recv_b, send_c, recv_c,
+):
+    n = nx * ny
+    me = lax.axis_index("gx") * ny + lax.axis_index("gy")
+
+    def place(peer):
+        return (peer // ny, peer % ny)
+
+    def remote(src, dst, send, recv, peer):
+        return pltpu.make_async_remote_copy(
+            src_ref=src, dst_ref=dst, send_sem=send, recv_sem=recv,
+            device_id=place(peer), device_id_type=pl.DeviceIdType.MESH)
+
+    def part_copy(k, peer, slot):
+        return remote(sums.at[peer], parts.at[slot], send_a.at[k], recv_a.at[slot], peer)
+
+    def block_copy(k, peer, slot):
+        return remote(block, blocks_ref.at[slot], send_b.at[k], recv_b.at[slot], peer)
+
+    def total_copy(k, peer, slot):
+        return remote(
+            total_ref.at[me], total_ref.at[slot], send_c.at[k], recv_c.at[slot], peer)
+
+    def peers(body):
+        @pl.loop(1, n)
+        def _(k):
+            body(k, lax.rem(me + k, n))
+
+    barrier = pltpu.get_barrier_semaphore()
+    peers(lambda k, peer: pl.semaphore_signal(
+        barrier, inc=1, device_id=place(peer), device_id_type=pl.DeviceIdType.MESH))
+    pl.semaphore_wait(barrier, n - 1)
+
+    peers(lambda k, peer: part_copy(k, peer, me).start())
+    peers(lambda k, peer: block_copy(k, peer, me).start())
+    blocks_ref[me] = block[...]
+
+    def add(k, total):
+        peer = lax.rem(me + k, n)
+        part_copy(k, peer, peer).wait_recv()
+        return total + parts[peer]
+
+    total_ref[me] = lax.fori_loop(1, n, add, sums[me])
+    peers(lambda k, peer: total_copy(k, peer, me).start())
+    peers(lambda k, peer: block_copy(k, peer, peer).wait_recv())
+    peers(lambda k, peer: total_copy(k, peer, peer).wait_recv())
+    peers(lambda k, peer: part_copy(k, peer, me).wait_send())
+    peers(lambda k, peer: block_copy(k, peer, me).wait_send())
+    peers(lambda k, peer: total_copy(k, peer, me).wait_send())
+
+
+def exchange(nx, ny, block, sums):
+    n = nx * ny
+    part = sums.shape[0] // n
+    vmem = pl.BlockSpec(memory_space=pltpu.VMEM)
+    return pl.pallas_call(
+        functools.partial(exchange_kernel, nx, ny),
+        out_shape=(
+            jax.ShapeDtypeStruct((n, *block.shape), F32),
+            jax.ShapeDtypeStruct((n, part, 128), F32),
+        ),
+        in_specs=[vmem, vmem],
+        out_specs=(vmem, vmem),
+        scratch_shapes=[pltpu.VMEM((n, part, 128), F32)]
+        + [pltpu.SemaphoreType.DMA((n,))] * 6,
+        compiler_params=pltpu.CompilerParams(
+            collective_id=0, has_side_effects=True, vmem_limit_bytes=24 << 20),
+        name="exchange",
+    )(block, sums.reshape(n, part, 128))
 
 
 def cut(start, share, core_shapes, window, r0, first_sum, middle_rows, last_sum):
@@ -258,23 +367,28 @@
     return own_first + own_middle + own_last
 
 
-def per_device(devices, c1, c2, c3, dense, w, bias, wout, labels, bag, d1, d2, d3):
+def per_device(nx, ny, c1, c2, c3, dense, w, bias, wout, labels, bag, d1, d2, d3):
+    devices = nx * ny
     total = c1.size + c2.size + c3.size
     share = total // devices
     row = c2.shape[1]
     window = min(-(-share // row) + 1, c2.shape[0])
-    me = lax.axis_index(AXES)
-    start = me * share
+    start = (lax.axis_index("gx") * ny + lax.axis_index("gy")) * share
     r0 = jnp.clip((start - c1.size) // row, 0, c2.shape[0] - window)
-    digits = lax.all_gather(jnp.stack([bag, d1, d2, d3]), AXES, axis=1, tiled=True)
-    gp, gw, gv, gf, gl = local_part(
-        c1, c2, c3, dense, w, bias[None], wout[None], labels[None], bag, d1, d2, d3)
-    gp_all = lax.all_gather(gp, AXES, axis=0, tiled=True)
-    gw, gv, gf, gl = lax.psum((gw, gv, gf, gl), AXES)
-    rows = middle_part(window, r0[None], c1, c3, gp_all, digits)
+    block, sums = local_part(
+        devices, c1, c2, c3, dense, w, bias[None], wout[None], labels[None], bag, d1, d2, d3)
+    blocks, sums = exchange(nx, ny, block, sums)
+    rows = middle_part(window, dense.shape[0], d1.shape[1], r0[None], c1, c3, blocks)
+    sums = sums.reshape(-1, 128)
+    places, _ = places_of(c1.shape, c3.shape, w.shape)
+
+    def take(name, count):
+        return jnp.concatenate([sums[at:at + count] for at in places[name]], axis=1)
+
     core = cut(start, share, (c1.shape, c2.shape, c3.shape), window, r0,
-               gf.reshape(-1), rows.reshape(-1), gl.reshape(-1))
-    return core, jnp.concatenate([gw, gv], axis=0)
+               take("first", c1.shape[0]).reshape(-1), rows.reshape(-1),
+               take("last", c3.shape[0]).reshape(-1))
+    return core, jnp.concatenate([take("weight", w.shape[0]), take("vectors", 2)], axis=0)
 
 
 def one_hot(digits, count, kind):
@@ -384,13 +498,13 @@
 
 
 def solution(mesh):
-    devices = mesh.shape["gx"] * mesh.shape["gy"]
+    nx, ny = mesh.shape["gx"], mesh.shape["gy"]
     whole, split, rows = P(), P(AXES), P(AXES, None)
 
     def step(*args):
         cores, dense = args[:3], args[3]
         if dense.size < sum(core.size for core in cores):
-            body = functools.partial(per_device, devices)
+            body = functools.partial(per_device, nx, ny)
         else:
             body = per_device_dense
         return jax.shard_map(

time: 232 us -> 91.4 us (0.39)
  blocking collectives: 108 us -> 0 us
  waiting for transfers between devices: 79.8 us -> 0 us
  Pallas kernels: 15.1 us -> 79 us
  between operations: 14.2 us -> 0.78 us
    all_gather x1 -> x0, blocking collectives: 70.9 us -> none  [per_device(): lax.all_gather(jnp.stack([bag, d1, d2, d3]), AXES, axis=1, tiled=True)]
    pallas_call x2 -> x3, Pallas kernels: 15.1 us -> 79 us  [the longest x1 64.4 us: exchange(): pl.pallas_call(functools.partial(exchange_kernel, nx, ny), out_shape=(jax...]
    all_gather x1 -> x0, waiting for transfers between devices: 55.1 us -> none  [per_device(): gp_all = lax.all_gather(gp, AXES, axis=0, tiled=True)]
    psum x1 -> x0, blocking collectives: 36.9 us -> none  [per_device(): gw, gv, gf, gl = lax.psum((gw, gv, gf, gl), AXES)]
    psum x1 -> x0, waiting for transfers between devices: 24 us -> none  [per_device(): gw, gv, gf, gl = lax.psum((gw, gv, gf, gl), AXES)]
    unnamed x42 -> x28, local copies, waits for them, and re-layouts: 10.7 us -> 9.48 us
  transfers between devices with their start and end apart: 2 -> 0, of which waited for: 2 -> 0; matrix products, arithmetic and copies ran while one was open for 1% -> 0% of each run, Pallas kernels for 0% -> 0%
where the time goes in v2:
time: 91.4 us; the launch traced here: 91 us
  Pallas kernels  79 us (86%)
  local copies, waits for them, and re-layouts  9.55 us (10%)
  other arithmetic  1.63 us (2%)
    pallas_call x1, Pallas kernels, exchange(): pl.pallas_call(functools.partial(exchange_kernel, nx, ny), out_shape=(jax...  64.4 us
    unnamed x28, local copies, waits for them, and re-layouts  9.48 us
    pallas_call x1, Pallas kernels, local_part(): pl.pallas_call(local_kernel, out_shape=(shape(samples + up(4 * looks // 1...  8.26 us
    pallas_call x1, Pallas kernels, middle_part(): pl.pallas_call(functools.partial(middle_kernel, window, chunk, samples, l...  6.37 us

profile of v2, /device:TPU:0, one launch (start us, length us, event | category | flops | bytes accessed | tf_op | source)
XLA Modules:
  0.0 91.0 jit_solution(15755943230057997940)
XLA Ops:
  0.6 0.0 copy-start
  0.7 1.4 %copy-done = bf16[200,4096]{1,0:T(8,128)(2,1)S(1)} copy-done((bf16[200,4096]{1,0:T(8,128)(2,1)S(1)}, bf16[200,4096]{1,0:T(8,128)(2,1)}, u32[]{:S(2)}) %copy-start) | copy-done | bytes 1638424
  2.1 0.0 copy-start.1
  2.1 0.9 copy-done.1
  3.0 0.0 copy-start.3
  3.0 0.8 copy-done.3
  3.8 0.0 copy-start.5
  3.8 0.9 copy-done.5
  4.7 0.0 copy-start.6
  4.7 0.7 copy-done.6
  5.4 0.7 copy-done.7
  6.1 0.0 copy-start.8
  6.1 0.7 copy-done.8
  6.8 0.0 copy-start.9
  6.8 0.7 copy-done.9
  7.4 0.0 copy-start.10
  7.4 0.7 copy-done.10
  8.1 0.0 copy-start.11
  8.1 0.7 copy-done.11
  8.8 0.0 copy-start.12
  8.8 0.7 copy-done.12
  9.5 0.0 copy-start.13
  9.5 0.7 copy-done.13
  10.1 0.0 copy-start.2
  10.1 0.0 copy-start.4
  10.1 8.3 %local.1 = (f32[72,128]{1,0:T(8,128)S(1)}, f32[1280,128]{1,0:T(8,128)S(1)}) custom-call(bf16[200,128]{1,0:T(8,128)(2,1)S(1)} %copy-done.3, bf16[200,4096]{1,0:T(8,128)(2,1)S(1)} %copy-done, bf16[250,256]{1,0:T(8,128)(2,1)S(1)} %copy-done.1, bf16[64,128]{1,0:T(8,128)(2,1)S(1)} %copy-done.6, bf16[256,256]{1,0:T(8,128)(2,1)S(1)} %copy-done.5, ...), custom_call_target="tpu_custom_call" | custom-call | tf_op jit(solution)/shard_map/local/pallas_call | solution.py:180
  18.4 64.4 %exchange.1 = (f32[32,72,128]{2,1,0:T(8,128)S(1)}, f32[32,40,128]{2,1,0:T(8,128)S(1)}) custom-call(f32[72,128]{1,0:T(8,128)S(1)} %get-tuple-element.6.block, f32[32,40,128]{2,1,0:T(8,128)S(1)} %bitcast.9), custom_call_target="tpu_custom_call" | custom-call | tf_op jit(solution)/shard_map/exchange/pallas_call | solution.py:339
  82.8 0.0 copy-done.2
  82.9 0.0 copy-done.4
  82.9 6.4 %middle.1 = f32[256,128]{1,0:T(8,128)S(1)} custom-call(s32[1]{0:T(128)} %bitcast.6.r0_ref, bf16[200,128]{1,0:T(8,128)(2,1)S(1)} %copy-done.4, bf16[250,256]{1,0:T(8,128)(2,1)S(1)} %copy-done.2, f32[32,72,128]{2,1,0:T(8,128)S(1)} %get-tuple-element.9.blocks), custom_call_target="tpu_custom_call" | custom-call | tf_op jit(solution)/shard_map/middle/pallas_call | solution.py:265
  89.3 0.9 fusion.1
  90.2 0.7 maximum_maximum_fusion
  (7 shorter events, 0.1 us)
Async XLA Ops:
  0.6 1.4 %copy-start = (bf16[200,4096]{1,0:T(8,128)(2,1)S(1)}, bf16[200,4096]{1,0:T(8,128)(2,1)}, u32[]{:S(2)}) copy-start(bf16[200,4096]{1,0:T(8,128)(2,1)} %c2.1) | copy-start | bytes 4915204
  2.1 0.9 copy-start.1
  3.0 0.8 copy-start.3
  3.8 0.9 copy-start.5
  4.7 0.7 copy-start.6
  5.4 0.7 copy-start.7
  6.1 0.7 copy-start.8
  6.8 0.7 copy-start.9
  7.4 0.7 copy-start.10
  8.1 0.7 copy-start.11
  8.8 0.7 copy-start.12
  9.5 0.7 copy-start.13
  10.1 72.7 %copy-start.2 = (bf16[250,256]{1,0:T(8,128)(2,1)S(1)}, bf16[250,256]{1,0:T(8,128)(2,1)}, u32[]{:S(2)}) copy-start(bf16[250,256]{1,0:T(8,128)(2,1)} %c3.3) | copy-start | bytes 384004
  10.1 72.7 %copy-start.4 = (bf16[200,128]{1,0:T(8,128)(2,1)S(1)}, bf16[200,128]{1,0:T(8,128)(2,1)}, u32[]{:S(2)}) copy-start(bf16[200,128]{1,0:T(8,128)(2,1)} %c1.3) | copy-start | bytes 153604

commit v3 on v2

--- a/solution.py
+++ b/solution.py
@@ -173,20 +173,36 @@
     put("last", 0, dot(hot3.astype(F32), gl_s[...], across, HIGH))
 
 
+def fetch_then(count, kernel, *refs):
+    inputs, rest = refs[:count], refs[count:-count - 1]
+    held, sems = refs[-count - 1:-1], refs[-1]
+    copies = [
+        pltpu.make_async_copy(inputs[k], held[k], sems.at[k]) for k in range(count)]
+    for copy in copies:
+        copy.start()
+    for copy in copies:
+        copy.wait()
+    kernel(*held, *rest)
+
+
 def local_part(devices, c1, c2, c3, dense, w, bias, wout, labels, bag, d1, d2, d3):
     samples, looks = dense.shape[0], d1.shape[1]
     shape = lambda *dims: jax.ShapeDtypeStruct(dims, F32)
     scratch = [R * SIDE, D1 * R, R * D3, R * D3, D1 * SIDE, D1 * SIDE, WIDTH, WIDTH, D1 * R, R * D3]
+    inputs = (c1, c2, c3, dense, w, bias, wout, labels, bag, d1, d2, d3)
     return pl.pallas_call(
-        local_kernel,
+        functools.partial(fetch_then, len(inputs), local_kernel),
+        in_specs=[pl.BlockSpec(memory_space=pltpu.HBM)] * len(inputs),
         out_shape=(
             shape(samples + up(4 * looks // 128, 8), WIDTH),
             shape(up(places_of(c1.shape, c3.shape, w.shape)[1], 8 * devices), 128),
         ),
-        scratch_shapes=[pltpu.VMEM((rows, looks), F32) for rows in scratch],
+        scratch_shapes=[pltpu.VMEM((rows, looks), F32) for rows in scratch]
+        + [pltpu.VMEM(x.shape, x.dtype) for x in inputs]
+        + [pltpu.SemaphoreType.DMA((len(inputs),))],
         compiler_params=pltpu.CompilerParams(vmem_limit_bytes=40 << 20),
         name="local",
-    )(c1, c2, c3, dense, w, bias, wout, labels, bag, d1, d2, d3)
+    )(*inputs)
 
 
 def middle_kernel(
@@ -279,77 +295,138 @@
     )(r0, c1, c3, blocks)
 
 
+def levels(nx, ny):
+    cores = 2 if nx % 2 == 0 else 1
+    return cores, nx // cores, ny
+
+
 def exchange_kernel(
     nx, ny, block, sums, blocks_ref, total_ref,
-    parts, send_a, recv_a, send_b, recv_b, send_c, recv_c,
+    part0, part1, part2, acc0, acc1, *sems,
 ):
-    n = nx * ny
-    me = lax.axis_index("gx") * ny + lax.axis_index("gy")
-
-    def place(peer):
-        return (peer // ny, peer % ny)
-
-    def remote(src, dst, send, recv, peer):
+    cores, chips, planes = levels(nx, ny)
+    gx, plane = lax.axis_index("gx"), lax.axis_index("gy")
+    core, chip = gx % cores, gx // cores
+
+    def on_core(k):
+        return (chip * cores + (core + k) % cores, plane)
+
+    def on_chip(k):
+        return (((chip + k) % chips) * cores + core, plane)
+
+    def on_plane(k):
+        return (gx, (plane + k) % planes)
+
+    def remote(src, dst, number, k, peer):
         return pltpu.make_async_remote_copy(
-            src_ref=src, dst_ref=dst, send_sem=send, recv_sem=recv,
-            device_id=place(peer), device_id_type=pl.DeviceIdType.MESH)
-
-    def part_copy(k, peer, slot):
-        return remote(sums.at[peer], parts.at[slot], send_a.at[k], recv_a.at[slot], peer)
-
-    def block_copy(k, peer, slot):
-        return remote(block, blocks_ref.at[slot], send_b.at[k], recv_b.at[slot], peer)
-
-    def total_copy(k, peer, slot):
-        return remote(
-            total_ref.at[me], total_ref.at[slot], send_c.at[k], recv_c.at[slot], peer)
-
-    def peers(body):
-        @pl.loop(1, n)
-        def _(k):
-            body(k, lax.rem(me + k, n))
+            src_ref=src, dst_ref=dst,
+            send_sem=sems[2 * number].at[k], recv_sem=sems[2 * number + 1].at[k],
+            device_id=peer, device_id_type=pl.DeviceIdType.MESH)
+
+    def stage(number, size, copy):
+        for k in range(1, size):
+            copy(k, k).start()
+
+        def arrived():
+            for k in range(1, size):
+                copy(k, -k).wait_recv()
+
+        def sent():
+            for k in range(1, size):
+                copy(k, k).wait_send()
+
+        return arrived, sent
+
+    def spread(ref, number, size, mine, view, peer):
+        def copy(k, off):
+            at = mine if off > 0 else (mine + off + size) % size
+            return remote(view(ref, at), view(ref, at), number, k, peer(k))
+        return stage(number, size, copy)
 
     barrier = pltpu.get_barrier_semaphore()
-    peers(lambda k, peer: pl.semaphore_signal(
-        barrier, inc=1, device_id=place(peer), device_id_type=pl.DeviceIdType.MESH))
-    pl.semaphore_wait(barrier, n - 1)
-
-    peers(lambda k, peer: part_copy(k, peer, me).start())
-    peers(lambda k, peer: block_copy(k, peer, me).start())
-    blocks_ref[me] = block[...]
-
-    def add(k, total):
-        peer = lax.rem(me + k, n)
-        part_copy(k, peer, peer).wait_recv()
-        return total + parts[peer]
-
-    total_ref[me] = lax.fori_loop(1, n, add, sums[me])
-    peers(lambda k, peer: total_copy(k, peer, me).start())
-    peers(lambda k, peer: block_copy(k, peer, peer).wait_recv())
-    peers(lambda k, peer: total_copy(k, peer, peer).wait_recv())
-    peers(lambda k, peer: part_copy(k, peer, me).wait_send())
-    peers(lambda k, peer: block_copy(k, peer, me).wait_send())
-    peers(lambda k, peer: total_copy(k, peer, me).wait_send())
+    greeted = 0
+    for size, peer in ((cores, on_core), (chips, on_chip), (planes, on_plane)):
+        for k in range(1, size):
+            pl.semaphore_signal(
+                barrier, inc=1, device_id=peer(k), device_id_type=pl.DeviceIdType.MESH)
+            greeted += 1
+    pl.semaphore_wait(barrier, greeted)
+
+    sent = []
+
+    def go(pair):
+        sent.append(pair[1])
+        return pair[0]
+
+    def block_copy(k, off):
+        at = plane if off > 0 else (plane + off + planes) % planes
+        return remote(block, blocks_ref.at[core, chip, at], 3, k, on_plane(k))
+
+    arrived_r0 = go(stage(0, cores, lambda k, off: remote(
+        sums.at[(core + k) % cores], part0.at[k], 0, k, on_core(k))))
+    arrived_bz = go(stage(3, planes, block_copy))
+    blocks_ref[core, chip, plane] = block[...]
+
+    arrived_r0()
+    total = sums[core]
+    for k in range(1, cores):
+        total = total + part0[k]
+    acc0[...] = total
+    arrived_r1 = go(stage(1, chips, lambda k, off: remote(
+        acc0.at[(chip + k) % chips], part1.at[k], 1, k, on_chip(k))))
+    arrived_bz()
+    arrived_b1 = go(spread(
+        blocks_ref, 4, chips, chip, lambda r, at: r.at[core, at], on_chip))
+
+    arrived_r1()
+    total = acc0[chip]
+    for k in range(1, chips):
+        total = total + part1[k]
+    acc1[...] = total
+    arrived_r2 = go(stage(2, planes, lambda k, off: remote(
+        acc1.at[(plane + k) % planes], part2.at[k], 2, k, on_plane(k))))
+    arrived_r2()
+    total = acc1[plane]
+    for k in range(1, planes):
+        total = total + part2[k]
+    total_ref[core, chip, plane] = total
+    go(spread(
+        total_ref, 5, planes, plane, lambda r, at: r.at[core, chip, at], on_plane))()
+    arrived_a1 = go(spread(
+        total_ref, 6, chips, chip, lambda r, at: r.at[core, at], on_chip))
+    arrived_b1()
+    arrived_b0 = go(spread(blocks_ref, 7, cores, core, lambda r, at: r.at[at], on_core))
+    arrived_a1()
+    arrived_a0 = go(spread(total_ref, 8, cores, core, lambda r, at: r.at[at], on_core))
+    arrived_b0()
+    arrived_a0()
+    for wait in sent:
+        wait()
 
 
 def exchange(nx, ny, block, sums):
-    n = nx * ny
-    part = sums.shape[0] // n
+    cores, chips, planes = levels(nx, ny)
+    part = sums.shape[0] // (nx * ny)
     vmem = pl.BlockSpec(memory_space=pltpu.VMEM)
-    return pl.pallas_call(
+    shape = (cores, chips, planes, part, 128)
+    scratch = [
+        (cores, *shape[1:]), (chips, *shape[2:]), (planes, *shape[3:]), shape[1:], shape[2:]]
+    sizes = (cores, chips, planes, planes, chips, planes, chips, cores, cores)
+    blocks, total = pl.pallas_call(
         functools.partial(exchange_kernel, nx, ny),
         out_shape=(
-            jax.ShapeDtypeStruct((n, *block.shape), F32),
-            jax.ShapeDtypeStruct((n, part, 128), F32),
+            jax.ShapeDtypeStruct((cores, chips, planes, *block.shape), F32),
+            jax.ShapeDtypeStruct(shape, F32),
         ),
         in_specs=[vmem, vmem],
         out_specs=(vmem, vmem),
-        scratch_shapes=[pltpu.VMEM((n, part, 128), F32)]
-        + [pltpu.SemaphoreType.DMA((n,))] * 6,
+        scratch_shapes=[pltpu.VMEM(dims, F32) for dims in scratch]
+        + [pltpu.SemaphoreType.DMA((size,)) for size in sizes for _ in range(2)],
         compiler_params=pltpu.CompilerParams(
             collective_id=0, has_side_effects=True, vmem_limit_bytes=24 << 20),
         name="exchange",
-    )(block, sums.reshape(n, part, 128))
+    )(block, sums.reshape(shape))
+    return blocks.reshape(-1, *block.shape), total
 
 
 def cut(start, share, core_shapes, window, r0, first_sum, middle_rows, last_sum):

time: 91.4 us -> 54.6 us (0.60)
  Pallas kernels: 79 us -> 42.3 us
    pallas_call x1, Pallas kernels: 64.4 us -> 26.9 us  [exchange(): pl.pallas_call(functools.partial(exchange_kernel, nx, ny), out_shape=(jax...]
where the time goes in v3:
time: 54.6 us; the launch traced here: 54.2 us
  Pallas kernels  42.3 us (77%)
  local copies, waits for them, and re-layouts  9.55 us (17%)
  other arithmetic  1.63 us (3%)
  between operations  0.78 us (1%)
    pallas_call x1, Pallas kernels, exchange(): pl.pallas_call(functools.partial(exchange_kernel, nx, ny), out_shape=(jax...  26.9 us
    unnamed x28, local copies, waits for them, and re-layouts  9.48 us
    pallas_call x1, Pallas kernels, local_part(): pl.pallas_call(functools.partial(fetch_then, len(inputs), local_kernel),...  9 us
    pallas_call x1, Pallas kernels, middle_part(): pl.pallas_call(functools.partial(middle_kernel, window, chunk, samples, l...  6.37 us

profile of v3, /device:TPU:0, one launch (start us, length us, event | category | flops | bytes accessed | tf_op | source)
XLA Modules:
  0.0 54.2 jit_solution(7892231302021928173)
XLA Ops:
  0.6 0.0 copy-start
  0.7 1.4 %copy-done = bf16[200,4096]{1,0:T(8,128)(2,1)S(1)} copy-done((bf16[200,4096]{1,0:T(8,128)(2,1)S(1)}, bf16[200,4096]{1,0:T(8,128)(2,1)}, u32[]{:S(2)}) %copy-start) | copy-done | bytes 1638424
  2.1 0.0 copy-start.1
  2.1 0.9 %copy-done.1 = bf16[250,256]{1,0:T(8,128)(2,1)S(1)} copy-done((bf16[250,256]{1,0:T(8,128)(2,1)S(1)}, bf16[250,256]{1,0:T(8,128)(2,1)}, u32[]{:S(2)}) %copy-start.1) | copy-done | bytes 128024
  3.0 0.0 copy-start.3
  3.0 0.8 %copy-done.3 = bf16[200,128]{1,0:T(8,128)(2,1)S(1)} copy-done((bf16[200,128]{1,0:T(8,128)(2,1)S(1)}, bf16[200,128]{1,0:T(8,128)(2,1)}, u32[]{:S(2)}) %copy-start.3) | copy-done | bytes 51224
  3.8 0.0 copy-start.5
  3.8 0.9 %copy-done.5 = bf16[256,256]{1,0:T(8,128)(2,1)S(1)} copy-done((bf16[256,256]{1,0:T(8,128)(2,1)S(1)}, bf16[256,256]{1,0:T(8,128)(2,1)}, u32[]{:S(2)}) %copy-start.5) | copy-done | bytes 131096
  4.7 0.0 copy-start.6
  4.7 0.7 %copy-done.6 = bf16[64,128]{1,0:T(8,128)(2,1)S(1)} copy-done((bf16[64,128]{1,0:T(8,128)(2,1)S(1)}, bf16[64,128]{1,0:T(8,128)(2,1)}, u32[]{:S(2)}) %copy-start.6) | copy-done | bytes 16408
  5.4 0.0 copy-start.7
  5.4 0.7 %copy-done.7 = f32[256]{0:T(256)S(1)} copy-done((f32[256]{0:T(256)S(1)}, f32[256]{0:T(256)}, u32[]{:S(2)}) %copy-start.7) | copy-done | bytes 1048
  6.1 0.0 copy-start.8
  6.1 0.7 %copy-done.8 = f32[256]{0:T(256)S(1)} copy-done((f32[256]{0:T(256)S(1)}, f32[256]{0:T(256)}, u32[]{:S(2)}) %copy-start.8) | copy-done | bytes 1048
  6.8 0.0 copy-start.9
  6.8 0.7 %copy-done.9 = s32[1,256]{1,0:T(1,128)S(1)} copy-done((s32[1,256]{1,0:T(1,128)S(1)}, s32[1,256]{1,0:T(1,128)}, u32[]{:S(2)}) %copy-start.9) | copy-done | bytes 1048
  7.4 0.0 copy-start.10
  7.4 0.7 %copy-done.10 = s32[1,256]{1,0:T(1,128)S(1)} copy-done((s32[1,256]{1,0:T(1,128)S(1)}, s32[1,256]{1,0:T(1,128)}, u32[]{:S(2)}) %copy-start.10) | copy-done | bytes 1048
  8.1 0.0 copy-start.11
  8.1 0.7 %copy-done.11 = s32[1,256]{1,0:T(1,128)S(1)} copy-done((s32[1,256]{1,0:T(1,128)S(1)}, s32[1,256]{1,0:T(1,128)}, u32[]{:S(2)}) %copy-start.11) | copy-done | bytes 1048
  8.8 0.0 copy-start.12
  8.8 0.7 %copy-done.12 = s32[1,256]{1,0:T(1,128)S(1)} copy-done((s32[1,256]{1,0:T(1,128)S(1)}, s32[1,256]{1,0:T(1,128)}, u32[]{:S(2)}) %copy-start.12) | copy-done | bytes 1048
  9.5 0.0 copy-start.13
  9.5 0.7 %copy-done.13 = s32[64]{0:T(128)S(1)} copy-done((s32[64]{0:T(128)S(1)}, s32[64]{0:T(128)}, u32[]{:S(2)}) %copy-start.13) | copy-done | bytes 280
  10.1 0.0 copy-start.2
  10.1 9.0 %local.1 = (f32[72,128]{1,0:T(8,128)S(1)}, f32[1280,128]{1,0:T(8,128)S(1)}) custom-call(bf16[200,128]{1,0:T(8,128)(2,1)S(1)} %copy-done.3, bf16[200,4096]{1,0:T(8,128)(2,1)S(1)} %copy-done, bf16[250,256]{1,0:T(8,128)(2,1)S(1)} %copy-done.1, bf16[64,128]{1,0:T(8,128)(2,1)S(1)} %copy-done.6, bf16[256,256]{1,0:T(8,128)(2,1)S(1)} %copy-done.5, ...), custom_call_target="tpu_custom_call" | custom-call | tf_op jit(solution)/shard_map/local/pallas_call | solution.py:193
  19.1 26.9 %exchange.1 = (f32[2,4,4,72,128]{4,3,2,1,0:T(8,128)S(1)}, f32[2,4,4,40,128]{4,3,2,1,0:T(8,128)S(1)}) custom-call(f32[72,128]{1,0:T(8,128)S(1)} %get-tuple-element.6.block, f32[2,4,4,40,128]{4,3,2,1,0:T(8,128)S(1)} %bitcast.11), custom_call_target="tpu_custom_call" | custom-call | tf_op jit(solution)/shard_map/exchange/pallas_call | solution.py:415
  46.1 0.0 copy-done.2
  46.1 0.0 copy-done.4
  46.1 6.4 %middle.1 = f32[256,128]{1,0:T(8,128)S(1)} custom-call(s32[1]{0:T(128)} %bitcast.6.r0_ref, bf16[200,128]{1,0:T(8,128)(2,1)S(1)} %copy-done.4, bf16[250,256]{1,0:T(8,128)(2,1)S(1)} %copy-done.2, f32[32,72,128]{2,1,0:T(8,128)S(1)} %bitcast.10), custom_call_target="tpu_custom_call" | custom-call | tf_op jit(solution)/shard_map/middle/pallas_call | solution.py:281
  52.6 0.9 %fusion.1 = f32[28400]{0:T(1024)} fusion(s32[]{:T(128)S(6)} %select_n.10, f32[25600]{0:T(1024)S(1)} %slice_bitcast_fusion, s32[]{:T(128)S(6)} %min.15, f32[32768]{0:T(1024)S(1)} %bitcast.16, s32[]{:T(128)S(6)} %min.16, f32[64000]{0:T(1024)S(1)} %reshape.27), kind=kLoop, calls=%fused_computation.6 | loop fusion | flops 56800 | bytes 603084 | tf_op jit(solution)/shard_map/add | solution.py:444
  53.5 0.7 %maximum_maximum_fusion = f32[258,256]{1,0:T(8,128)} fusion(f32[2,128]{1,0:T(2,128)S(1)} %get-tuple-element.13, f32[2,128]{1,0:T(2,128)S(1)} %get-tuple-element.12, f32[256,128]{1,0:T(8,128)S(1)} %get-tuple-element.11, f32[256,128]{1,0:T(8,128)S(1)} %get-tuple-element.10), kind=kLoop, calls=%fused_computation.2 | loop fusion | flops 198144 | bytes 528384 | tf_op jit(solution)/shard_map/concatenate | solution.py:468
  (7 shorter events, 0.1 us)
Async XLA Ops:
  0.6 1.4 %copy-start = (bf16[200,4096]{1,0:T(8,128)(2,1)S(1)}, bf16[200,4096]{1,0:T(8,128)(2,1)}, u32[]{:S(2)}) copy-start(bf16[200,4096]{1,0:T(8,128)(2,1)} %refs_1_.1) | copy-start | bytes 4915204
  2.1 0.9 %copy-start.1 = (bf16[250,256]{1,0:T(8,128)(2,1)S(1)}, bf16[250,256]{1,0:T(8,128)(2,1)}, u32[]{:S(2)}) copy-start(bf16[250,256]{1,0:T(8,128)(2,1)} %c3.1) | copy-start | bytes 384004
  3.0 0.8 %copy-start.3 = (bf16[200,128]{1,0:T(8,128)(2,1)S(1)}, bf16[200,128]{1,0:T(8,128)(2,1)}, u32[]{:S(2)}) copy-start(bf16[200,128]{1,0:T(8,128)(2,1)} %c1.1) | copy-start | bytes 153604
  3.8 0.9 %copy-start.5 = (bf16[256,256]{1,0:T(8,128)(2,1)S(1)}, bf16[256,256]{1,0:T(8,128)(2,1)}, u32[]{:S(2)}) copy-start(bf16[256,256]{1,0:T(8,128)(2,1)} %refs_4_.1) | copy-start | bytes 393220
  4.7 0.7 %copy-start.6 = (bf16[64,128]{1,0:T(8,128)(2,1)S(1)}, bf16[64,128]{1,0:T(8,128)(2,1)}, u32[]{:S(2)}) copy-start(bf16[64,128]{1,0:T(8,128)(2,1)} %refs_3_.1) | copy-start | bytes 49156
  5.4 0.7 %copy-start.7 = (f32[256]{0:T(256)S(1)}, f32[256]{0:T(256)}, u32[]{:S(2)}) copy-start(f32[256]{0:T(256)} %param.17) | copy-start | bytes 3076
  6.1 0.7 %copy-start.8 = (f32[256]{0:T(256)S(1)}, f32[256]{0:T(256)}, u32[]{:S(2)}) copy-start(f32[256]{0:T(256)} %param.18) | copy-start | bytes 3076
  6.8 0.7 %copy-start.9 = (s32[1,256]{1,0:T(1,128)S(1)}, s32[1,256]{1,0:T(1,128)}, u32[]{:S(2)}) copy-start(s32[1,256]{1,0:T(1,128)} %refs_8_.1) | copy-start | bytes 3076
  7.4 0.7 %copy-start.10 = (s32[1,256]{1,0:T(1,128)S(1)}, s32[1,256]{1,0:T(1,128)}, u32[]{:S(2)}) copy-start(s32[1,256]{1,0:T(1,128)} %refs_9_.1) | copy-start | bytes 3076
  8.1 0.7 %copy-start.11 = (s32[1,256]{1,0:T(1,128)S(1)}, s32[1,256]{1,0:T(1,128)}, u32[]{:S(2)}) copy-start(s32[1,256]{1,0:T(1,128)} %refs_10_.1) | copy-start | bytes 3076
  8.8 0.7 %copy-start.12 = (s32[1,256]{1,0:T(1,128)S(1)}, s32[1,256]{1,0:T(1,128)}, u32[]{:S(2)}) copy-start(s32[1,256]{1,0:T(1,128)} %refs_11_.1) | copy-start | bytes 3076
  9.5 0.7 %copy-start.13 = (s32[64]{0:T(128)S(1)}, s32[64]{0:T(128)}, u32[]{:S(2)}) copy-start(s32[64]{0:T(128)} %param.19) | copy-start | bytes 772
  10.1 36.0 %copy-start.2 = (bf16[250,256]{1,0:T(8,128)(2,1)S(1)}, bf16[250,256]{1,0:T(8,128)(2,1)}, u32[]{:S(2)}) copy-start(bf16[250,256]{1,0:T(8,128)(2,1)} %c3.1) | copy-start | bytes 384004
  10.1 36.0 %copy-start.4 = (bf16[200,128]{1,0:T(8,128)(2,1)S(1)}, bf16[200,128]{1,0:T(8,128)(2,1)}, u32[]{:S(2)}) copy-start(bf16[200,128]{1,0:T(8,128)(2,1)} %c1.1) | copy-start | bytes 153604

commit v4 on v3

--- a/solution.py
+++ b/solution.py
@@ -200,7 +200,7 @@
         scratch_shapes=[pltpu.VMEM((rows, looks), F32) for rows in scratch]
         + [pltpu.VMEM(x.shape, x.dtype) for x in inputs]
         + [pltpu.SemaphoreType.DMA((len(inputs),))],
-        compiler_params=pltpu.CompilerParams(vmem_limit_bytes=40 << 20),
+        compiler_params=pltpu.CompilerParams(vmem_limit_bytes=60 * 1024 * 1024),
         name="local",
     )(*inputs)
 

time: 54.6 us -> 48.5 us (0.89)
  local copies, waits for them, and re-layouts: 9.55 us -> 1.92 us
  Pallas kernels: 42.3 us -> 43.9 us
    unnamed x28 -> x8, local copies, waits for them, and re-layouts: 9.48 us -> 1.86 us
    pallas_call x1, Pallas kernels: 9 us -> 10.7 us  [local_part(): pl.pallas_call(functools.partial(fetch_then, len(inputs), local_kernel),...]
where the time goes in v4:
time: 48.5 us; the launch traced here: 48.2 us
  Pallas kernels  43.9 us (91%)
  local copies, waits for them, and re-layouts  1.92 us (4%)
  other arithmetic  1.63 us (3%)
  between operations  0.78 us (2%)
    pallas_call x1, Pallas kernels, exchange(): pl.pallas_call(functools.partial(exchange_kernel, nx, ny), out_shape=(jax...  26.8 us
    pallas_call x1, Pallas kernels, local_part(): pl.pallas_call(functools.partial(fetch_then, len(inputs), local_kernel),...  10.7 us
    pallas_call x1, Pallas kernels, middle_part(): pl.pallas_call(functools.partial(middle_kernel, window, chunk, samples, l...  6.37 us
    unnamed x8, local copies, waits for them, and re-layouts  1.86 us

profile of v4, /device:TPU:0, one launch (start us, length us, event | category | flops | bytes accessed | tf_op | source)
XLA Modules:
  0.0 48.2 jit_solution(2794876395433336066)
XLA Ops:
  0.6 0.0 copy-start.2
  0.6 0.0 copy-start.1
  0.7 10.7 %local.1 = (f32[72,128]{1,0:T(8,128)}, f32[1280,128]{1,0:T(8,128)}) custom-call(bf16[200,128]{1,0:T(8,128)(2,1)} %c1.1, bf16[200,4096]{1,0:T(8,128)(2,1)} %refs_1_.1, bf16[250,256]{1,0:T(8,128)(2,1)} %c3.1, bf16[64,128]{1,0:T(8,128)(2,1)} %refs_3_.1, bf16[256,256]{1,0:T(8,128)(2,1)} %refs_4_.1, f32[1,256]{1,0:T(1,128)} %bitcast.17, f32[1,256]{1,0:T(1,128)} %bitcast.18, ...), custom_call_target="tpu_custom_call" | custom-call | tf_op jit(solution)/shard_map/local/pallas_call | solution.py:193
  11.4 0.0 copy-start
  11.4 1.1 %copy-done = f32[1280,128]{1,0:T(8,128)S(1)} copy-done((f32[1280,128]{1,0:T(8,128)S(1)}, f32[1280,128]{1,0:T(8,128)}, u32[]{:S(2)}) %copy-start) | copy-done | bytes 655384
  12.5 0.0 copy-start.3
  12.5 0.8 %copy-done.3 = f32[72,128]{1,0:T(8,128)S(1)} copy-done((f32[72,128]{1,0:T(8,128)S(1)}, f32[72,128]{1,0:T(8,128)}, u32[]{:S(2)}) %copy-start.3) | copy-done | bytes 36888
  13.3 26.8 %exchange.1 = (f32[2,4,4,72,128]{4,3,2,1,0:T(8,128)S(1)}, f32[2,4,4,40,128]{4,3,2,1,0:T(8,128)S(1)}) custom-call(f32[72,128]{1,0:T(8,128)S(1)} %copy-done.3, f32[2,4,4,40,128]{4,3,2,1,0:T(8,128)S(1)} %bitcast.11), custom_call_target="tpu_custom_call" | custom-call | tf_op jit(solution)/shard_map/exchange/pallas_call | solution.py:415
  40.1 0.0 copy-done.2
  40.1 0.0 copy-done.1
  40.2 6.4 %middle.1 = f32[256,128]{1,0:T(8,128)S(1)} custom-call(s32[1]{0:T(128)} %bitcast.6.r0_ref, bf16[200,128]{1,0:T(8,128)(2,1)S(1)} %copy-done.2, bf16[250,256]{1,0:T(8,128)(2,1)S(1)} %copy-done.1, f32[32,72,128]{2,1,0:T(8,128)S(1)} %bitcast.10), custom_call_target="tpu_custom_call" | custom-call | tf_op jit(solution)/shard_map/middle/pallas_call | solution.py:281
  46.6 0.9 %fusion.1 = f32[28400]{0:T(1024)} fusion(s32[]{:T(128)S(6)} %select_n.10, f32[25600]{0:T(1024)S(1)} %slice_bitcast_fusion, s32[]{:T(128)S(6)} %min.15, f32[32768]{0:T(1024)S(1)} %bitcast.16, s32[]{:T(128)S(6)} %min.16, f32[64000]{0:T(1024)S(1)} %reshape.27), kind=kLoop, calls=%fused_computation.6 | loop fusion | flops 56800 | bytes 603084 | tf_op jit(solution)/shard_map/add | solution.py:444
  47.5 0.7 %maximum_maximum_fusion = f32[258,256]{1,0:T(8,128)} fusion(f32[2,128]{1,0:T(2,128)S(1)} %get-tuple-element.13, f32[2,128]{1,0:T(2,128)S(1)} %get-tuple-element.12, f32[256,128]{1,0:T(8,128)S(1)} %get-tuple-element.11, f32[256,128]{1,0:T(8,128)S(1)} %get-tuple-element.10), kind=kLoop, calls=%fused_computation.2 | loop fusion | flops 198144 | bytes 528384 | tf_op jit(solution)/shard_map/concatenate | solution.py:468
  (6 shorter events, 0.1 us)
Async XLA Ops:
  0.6 39.5 %copy-start.2 = (bf16[200,128]{1,0:T(8,128)(2,1)S(1)}, bf16[200,128]{1,0:T(8,128)(2,1)}, u32[]{:S(2)}) copy-start(bf16[200,128]{1,0:T(8,128)(2,1)} %c1.1) | copy-start | bytes 153604
  0.6 39.5 %copy-start.1 = (bf16[250,256]{1,0:T(8,128)(2,1)S(1)}, bf16[250,256]{1,0:T(8,128)(2,1)}, u32[]{:S(2)}) copy-start(bf16[250,256]{1,0:T(8,128)(2,1)} %c3.1) | copy-start | bytes 384004
  11.4 1.1 %copy-start = (f32[1280,128]{1,0:T(8,128)S(1)}, f32[1280,128]{1,0:T(8,128)}, u32[]{:S(2)}) copy-start(f32[1280,128]{1,0:T(8,128)} %get-tuple-element.7) | copy-start | bytes 1966084
  12.5 0.8 %copy-start.3 = (f32[72,128]{1,0:T(8,128)S(1)}, f32[72,128]{1,0:T(8,128)}, u32[]{:S(2)}) copy-start(f32[72,128]{1,0:T(8,128)} %get-tuple-element.6.block) | copy-start | bytes 110596
